TPU v7x, 256 devices: a whole 4x4x8 slice. The times are simulated.
256 devices in a mesh: section: 2 (over x_hi), feat: 16 (over y, x_lo, core), width: 8 (over z).
Axes of the slice: x: 4 (x_hi: 2, x_lo: 2; x = x_hi * 2 + x_lo), y: 4, z: 8, core: 2. Of those that a mesh axis runs over, the one named last changes fastest.
Arguments:
- mlp_inputs: bfloat16 [4, 1024, 2304], P('section', 'width'), may hold values from -6 to 6
- encoder: bfloat16 [4, 2304, 16384], P('section', 'width', 'feat'), may hold values from -0.125 to 0.125
- enc_bias: float32 [4, 16384], P('section', 'feat'), may hold values from -3 to 3
- decoder: bfloat16 [10, 16384, 2304], P('section', 'feat', 'width'), may hold values from -0.046875 to 0.046875
- dec_bias: float32 [4, 2304], P(None, 'width'), may hold values from -3 to 3
- targets: bfloat16 [4, 1024, 2304], P(None, None, 'width'), may hold values from -6 to 6
- live_rows: int32 [1024], replicated, may hold values 0 or 1
Outputs:
- errors: bfloat16 [4, 1024, 2304], P(None, None, 'width')
- gradients: bfloat16 [10, 16384, 2304], P('section', 'feat', 'width')
All inputs are finite; a program needn't handle non-finite values.
Results may differ from a plain program's by a relative error of at most 0.0042.
Values may be sent and summed in bfloat16 or wider, within the bound.
No kernel may reach another device: no remote copies, remote signals or barrier semaphores. Data moves between devices by JAX's collectives and lax.ppermute only.
A program may use at most 128 MiB of HBM per device.

v0:
```python
import jax
import jax.numpy as jnp
from jax import lax
from jax.sharding import PartitionSpec as P


def from_behind(value, axis, steps):
    count = lax.axis_size(axis)
    initial, last = (max(0, -steps), min(count, count - steps))
    return lax.ppermute(value, axis, [(source, source + steps) for source in range(initial, last)])


def pair_tables(layer_count):
    source_ids = []
    target_ids = []
    for source in range(layer_count):
        for target in range(source, layer_count):
            source_ids.append(source)
            target_ids.append(target)
    return (jnp.array(source_ids, jnp.int32), jnp.array(target_ids, jnp.int32))


def local(mlp_inputs, encoder, enc_bias, decoder, dec_bias, targets, live_rows):
    layers_here, tok_local, model_width = mlp_inputs.shape
    pre_act = jnp.einsum(
        "ltd,ldf->tlf",
        mlp_inputs,
        lax.all_gather(encoder, "width", axis=1, tiled=True),
        preferred_element_type=jnp.float32,
    )
    local_feats = jnp.maximum(pre_act + enc_bias[None, :, :], 0.0).astype(jnp.bfloat16)
    token_feats = lax.all_gather(local_feats, "width", axis=0, tiled=True)
    layers_all = dec_bias.shape[0]
    tokens_all = live_rows.shape[0]
    per_section = decoder.shape[0]
    source_ids, target_ids = pair_tables(layers_all)
    section_id = lax.axis_index("section")
    earlier = from_behind(token_feats[:, layers_here - 1], "section", 1)
    features = jnp.concatenate([earlier[:, None, :], token_feats], axis=1)
    first_layer = section_id * layers_here - 1
    rebuilt = jnp.zeros((layers_all, tokens_all, decoder.shape[2]), jnp.float32)
    chosen = []
    for pair_slot in range(per_section):
        pair_id = section_id * per_section + pair_slot
        source = source_ids[pair_id]
        target = target_ids[pair_id]
        picked = lax.dynamic_index_in_dim(features, source - first_layer, 1, keepdims=False)
        chosen.append((picked, target))
        partial_value = jnp.dot(picked, decoder[pair_slot], preferred_element_type=jnp.float32)
        current = lax.dynamic_index_in_dim(rebuilt, target, 0, keepdims=False)
        rebuilt = lax.dynamic_update_index_in_dim(rebuilt, current + partial_value, target, 0)
    summed = lax.psum(rebuilt, ("section", "feat"))
    keep_rows = live_rows.astype(jnp.float32)[None, :, None]
    errors = ((summed + dec_bias[:, None, :] - targets.astype(jnp.float32)) * keep_rows).astype(
        jnp.bfloat16
    )
    gradients = []
    for picked, target in chosen:
        residual = lax.dynamic_index_in_dim(errors, target, 0, keepdims=False)
        product = lax.dot_general(
            picked, residual, (((0,), (0,)), ((), ())), preferred_element_type=jnp.float32
        )
        gradients.append((product / tokens_all).astype(jnp.bfloat16))
    return (errors, jnp.stack(gradients))


def solution(mesh):
    placed = (
        P("section", "width", None),
        P("section", "width", "feat"),
        P("section", "feat"),
        P("section", "feat", "width"),
        P(None, "width"),
        P(None, None, "width"),
        P(),
    )
    return jax.shard_map(
        local,
        mesh=mesh,
        in_specs=placed,
        out_specs=(P(None, None, "width"), P("section", "feat", "width")),
        check_vma=False,
    )
```

profile of v0, /device:TPU:1, one launch (start us, length us, event | category | flops | bytes accessed | tf_op | source)
XLA Modules:
  0.0 397.8 jit_solution(8431505922366384273)
XLA Ops:
  8.0 109.4 %all-gather.3.cloned.1.call-done = bf16[2,2304,1024]{2,1,0:T(8,128)(2,1)} async-done(((bf16[2,288,1024]{2,1,0:T(8,128)(2,1)}), bf16[2,2304,1024]{2,1,0:T(8,128)(2,1)}) %all-gather.3.cloned.1.call-update) | async-done | bytes 9437200 | tf_op jit(solution)/shard_map/all_gather | solution.py:28
  117.3 7.3 %fusion.36 = bf16[128,2,1024]{0,2,1:T(8,128)(2,1)} fusion(bf16[2,2304,1024]{2,1,0:T(8,128)(2,1)} %all-gather.3.cloned.1.call-done, bf16[2,128,2304]{2,1,0:T(8,128)(2,1)S(1)} %copy-done, f32[2,1024]{1,0:T(2,128)} %param.11), kind=kOutput, calls=%fused_computation.59 | convolution fusion | flops 1208745984 | bytes 11149312 | tf_op jit(solution)/shard_map/ltd,ldf->tlf/dot_general | solution.py:25
  124.7 57.6 %all-gather.5.cloned.1.call-done = bf16[1024,2,1024]{0,2,1:T(8,128)(2,1)} async-done(((bf16[128,2,1024]{0,2,1:T(8,128)(2,1)}), bf16[1024,2,1024]{0,2,1:T(8,128)(2,1)}) %all-gather.5.cloned.1.call-update) | async-done | bytes 4194320 | tf_op jit(solution)/shard_map/all_gather | solution.py:32
  182.4 3.1 slice_bitcast_fusion
  185.4 4.4 %collective-permute-start = (bf16[1024,1024]{0,1:T(8,128)(2,1)}, bf16[1024,1024]{0,1:T(8,128)(2,1)S(1)}, u32[]{:S(2)}, u32[]{:S(2)}) collective-permute-start(bf16[1024,1024]{0,1:T(8,128)(2,1)} %slice_bitcast_fusion), channel_id=1, source_target_pairs={{0,128},{1,129},{2,130},{3,131},{4,132},{5,133},{6,134},{7,135},{8... | collective-permute-start | bytes 6291464 | tf_op jit(solution)/shard_map/ppermute | solution.py:10
  203.2 26.7 %collective-permute-done = bf16[1024,1024]{0,1:T(8,128)(2,1)S(1)} collective-permute-done((bf16[1024,1024]{0,1:T(8,128)(2,1)}, bf16[1024,1024]{0,1:T(8,128)(2,1)S(1)}, u32[]{:S(2)}, u32[]{:S(2)}) %collective-permute-start) | collective-permute-done | bytes 2097184 | tf_op jit(solution)/shard_map/ppermute | solution.py:10
  229.9 3.0 broadcast_in_dim.25
  233.7 3.4 fusion.18
  237.1 1.3 constant_dynamic-slice_fusion.3
  238.5 2.2 fusion.17
  240.7 1.3 constant_dynamic-slice_fusion.2
  242.1 2.2 fusion.15
  244.3 1.3 constant_dynamic-slice_fusion.1
  245.6 2.3 fusion.13
  247.9 1.3 constant_dynamic-slice_fusion
  249.3 2.2 fusion.11
  252.2 126.4 %all-reduce.2.cloned.1.call-done = f32[4,1024,288]{1,2,0:T(8,128)} async-done(((f32[4,1024,288]{1,2,0:T(8,128)}), f32[4,1024,288]{1,2,0:T(8,128)}) %all-reduce.2.cloned.1.call-update) | async-done | bytes 4718608 | tf_op jit(solution)/shard_map/psum | solution.py:52
  378.6 3.9 multiply_convert_fusion
  382.8 1.4 fusion.35
  384.2 1.4 fusion.33
  385.6 1.4 fusion.31
  386.9 1.4 fusion.29
  388.3 1.4 fusion.27
  389.7 1.6 copy-done.9
  (27 shorter events, 3.4 us)
Async XLA Ops:
  7.2 110.2 %copy-start = (bf16[2,128,2304]{2,1,0:T(8,128)(2,1)S(1)}, bf16[2,128,2304]{2,1,0:T(8,128)(2,1)}, u32[]{:S(2)}) copy-start(bf16[2,128,2304]{2,1,0:T(8,128)(2,1)} %param.9) | copy-start | bytes 3538948
  7.2 110.2 %all-gather.3.cloned.1.call-start = ((), (), s32[]{:S(2)}) async-start(), calls=%async_computation | async-start | bytes 10616832 | tf_op jit(solution)/shard_map/all_gather | solution.py:28
  7.9 174.4 %all-gather.5.cloned.1.call-start = ((), (), s32[]{:S(2)}) async-start(), calls=%async_computation.1 | async-start | bytes 4718592 | tf_op jit(solution)/shard_map/all_gather | solution.py:32
  124.7 65.2 %copy-start.5 = (s32[10]{0:T(128)S(1)}, s32[10]{0:T(128)}, u32[]{:S(2)}) copy-start(s32[10]{0:T(128)} %constant.92.clone) | copy-start | bytes 124
  124.7 65.2 %copy-start.6 = (s32[10]{0:T(128)S(1)}, s32[10]{0:T(128)}, u32[]{:S(2)}) copy-start(s32[10]{0:T(128)} %constant.93.clone) | copy-start | bytes 124
  124.7 253.9 %all-reduce.2.cloned.1.call-start = ((), (), s32[]{:S(2)}) async-start(), calls=%async_computation.2 | async-start | bytes 9437184 | tf_op jit(solution)/shard_map/psum | solution.py:52
  185.4 44.5 %collective-permute-start = (bf16[1024,1024]{0,1:T(8,128)(2,1)}, bf16[1024,1024]{0,1:T(8,128)(2,1)S(1)}, u32[]{:S(2)}, u32[]{:S(2)}) collective-permute-start(bf16[1024,1024]{0,1:T(8,128)(2,1)} %slice_bitcast_fusion), channel_id=1, source_target_pairs={{0,128},{1,129},{2,130},{3,131},{4,132},{5,133},{6,134},{7,135},{8... | collective-permute-start | bytes 6291464 | tf_op jit(solution)/shard_map/ppermute | solution.py:10
  229.9 3.8 copy-start.1
  233.7 4.7 %copy-start.3 = (bf16[5,1024,288]{1,2,0:T(8,128)(2,1)S(1)}, bf16[5,1024,288]{1,2,0:T(8,128)(2,1)}, u32[]{:S(2)}) copy-start(bf16[5,1024,288]{1,2,0:T(8,128)(2,1)} %param.12) | copy-start | bytes 8847364
  251.5 0.7 copy-start.8
  251.5 127.1 %copy-start.7 = (f32[4,288]{1,0:T(4,128)S(1)}, f32[4,288]{1,0:T(4,128)}, u32[]{:S(2)}) copy-start(f32[4,288]{1,0:T(4,128)} %param.13) | copy-start | bytes 13828
  378.6 4.2 %copy-start.2 = (bf16[1024,2,1024]{0,2,1:T(8,128)(2,1)S(1)}, bf16[1024,2,1024]{0,2,1:T(8,128)(2,1)}, u32[]{:S(2)}) copy-start(bf16[1024,2,1024]{0,2,1:T(8,128)(2,1)} %all-gather.5.cloned.1.call-done) | copy-start | bytes 12582916
  382.8 5.5 %copy-start.4 = (bf16[4,1024,288]{1,2,0:T(8,128)(2,1)}, bf16[4,1024,288]{1,2,0:T(8,128)(2,1)S(1)}, u32[]{:S(2)}) copy-start(bf16[4,1024,288]{1,2,0:T(8,128)(2,1)S(1)} %multiply_convert_fusion) | copy-start | bytes 7077892
  389.7 1.6 copy-start.9
Sparse Core Ops, SparseCore 0:
  9.8 107.5 all-gather.2
  124.8 57.5 all-gather.4
  251.6 126.9 all-reduce.1
where the time goes:
time: 398 us
  waiting for transfers between devices  321 us (81%)
  matrix products  26.5 us (7%)
  between operations  26.5 us (7%)
  local copies, waits for them, and re-layouts  15.5 us (4%)
  starting transfers between devices  4.52 us (1%)
    psum x1, waiting for transfers between devices, local(): summed = lax.psum(rebuilt, ('section', 'feat'))  126 us
    all_gather x1, waiting for transfers between devices, local(): lax.all_gather(encoder, 'width', axis=1, tiled=True)  109 us
    all_gather x1, waiting for transfers between devices, local(): token_feats = lax.all_gather(local_feats, 'width', axis=0, tiled=True)  57.6 us
    ppermute x1, waiting for transfers between devices, from_behind(): lax.ppermute(value, axis, [(source, source + steps) for source in range(i...  26.7 us
    dot_general x5, matrix products, local(): jnp.dot(picked, decoder[pair_slot], preferred_element_type=jnp.float32)  12.3 us
  transfers between devices with their start and end apart: 4, of which 4 were waited for; matrix products, arithmetic and copies ran while one was open for 0% of the time, Pallas kernels for 0%

commit v1 on v0

--- a/solution.py
+++ b/solution.py
@@ -49,7 +49,8 @@
         partial_value = jnp.dot(picked, decoder[pair_slot], preferred_element_type=jnp.float32)
         current = lax.dynamic_index_in_dim(rebuilt, target, 0, keepdims=False)
         rebuilt = lax.dynamic_update_index_in_dim(rebuilt, current + partial_value, target, 0)
-    summed = lax.psum(rebuilt, ("section", "feat"))
+    inner = lax.psum(rebuilt, "section")
+    summed = lax.psum(inner, "feat")
     keep_rows = live_rows.astype(jnp.float32)[None, :, None]
     errors = ((summed + dec_bias[:, None, :] - targets.astype(jnp.float32)) * keep_rows).astype(
         jnp.bfloat16

time: 398 us -> 553 us (1.39)
  waiting for transfers between devices: 321 us -> 475 us
    psum x1 -> x2, waiting for transfers between devices: 126 us -> 281 us  [the longest x1 144 us: local(): summed = lax.psum(inner, 'feat')]
  transfers between devices with their start and end apart: 4 -> 5, of which waited for: 4 -> 5; matrix products, arithmetic and copies ran while one was open for 0% -> 0% of each run, Pallas kernels for 0% -> 0%
where the time goes in v1:
time: 553 us; the launch traced here: 552 us
  waiting for transfers between devices  475 us (86%)
  matrix products  26.5 us (5%)
  between operations  26.5 us (5%)
  local copies, waits for them, and re-layouts  15.5 us (3%)
    psum x1, waiting for transfers between devices, local(): summed = lax.psum(inner, 'feat')  144 us
    psum x1, waiting for transfers between devices, local(): inner = lax.psum(rebuilt, 'section')  136 us
    all_gather x1, waiting for transfers between devices, local(): lax.all_gather(encoder, 'width', axis=1, tiled=True)  109 us
    all_gather x1, waiting for transfers between devices, local(): token_feats = lax.all_gather(local_feats, 'width', axis=0, tiled=True)  57.6 us
    ppermute x1, waiting for transfers between devices, from_behind(): lax.ppermute(value, axis, [(source, source + steps) for source in range(i...  26.9 us
    dot_general x5, matrix products, local(): jnp.dot(picked, decoder[pair_slot], preferred_element_type=jnp.float32)  12.3 us
  transfers between devices with their start and end apart: 5, of which 5 were waited for; matrix products, arithmetic and copies ran while one was open for 0% of the time, Pallas kernels for 0%

profile of v1, /device:TPU:1, one launch (start us, length us, event | category | flops | bytes accessed | tf_op | source)
XLA Modules:
  0.0 552.2 jit_solution(10342985006708061985)
XLA Ops:
  8.0 109.4 %all-gather.3.cloned.1.call-done = bf16[2,2304,1024]{2,1,0:T(8,128)(2,1)} async-done(((bf16[2,288,1024]{2,1,0:T(8,128)(2,1)}), bf16[2,2304,1024]{2,1,0:T(8,128)(2,1)}) %all-gather.3.cloned.1.call-update) | async-done | bytes 9437200 | tf_op jit(solution)/shard_map/all_gather | solution.py:28
  117.3 7.3 %fusion.36 = bf16[128,2,1024]{0,2,1:T(8,128)(2,1)} fusion(bf16[2,2304,1024]{2,1,0:T(8,128)(2,1)} %all-gather.3.cloned.1.call-done, bf16[2,128,2304]{2,1,0:T(8,128)(2,1)S(1)} %copy-done, f32[2,1024]{1,0:T(2,128)} %param.11), kind=kOutput, calls=%fused_computation.59 | convolution fusion | flops 1208745984 | bytes 11149312 | tf_op jit(solution)/shard_map/ltd,ldf->tlf/dot_general | solution.py:25
  124.7 57.6 %all-gather.5.cloned.1.call-done = bf16[1024,2,1024]{0,2,1:T(8,128)(2,1)} async-done(((bf16[128,2,1024]{0,2,1:T(8,128)(2,1)}), bf16[1024,2,1024]{0,2,1:T(8,128)(2,1)}) %all-gather.5.cloned.1.call-update) | async-done | bytes 4194320 | tf_op jit(solution)/shard_map/all_gather | solution.py:32
  182.4 3.1 slice_bitcast_fusion
  185.4 4.2 collective-permute-start
  203.0 26.9 %collective-permute-done = bf16[1024,1024]{0,1:T(8,128)(2,1)S(1)} collective-permute-done((bf16[1024,1024]{0,1:T(8,128)(2,1)}, bf16[1024,1024]{0,1:T(8,128)(2,1)S(1)}, u32[]{:S(2)}, u32[]{:S(2)}) %collective-permute-start) | collective-permute-done | bytes 2097184 | tf_op jit(solution)/shard_map/ppermute | solution.py:10
  229.9 3.0 broadcast_in_dim.25
  233.7 3.4 fusion.18
  237.1 1.3 constant_dynamic-slice_fusion.3
  238.5 2.2 fusion.17
  240.7 1.3 constant_dynamic-slice_fusion.2
  242.1 2.2 fusion.15
  244.3 1.3 constant_dynamic-slice_fusion.1
  245.6 2.3 fusion.13
  249.3 2.2 fusion.11
  251.7 136.4 %all-reduce.3.cloned.1.call-done = f32[4,1024,288]{1,2,0:T(8,128)} async-done(((f32[4,1024,288]{1,2,0:T(8,128)}), f32[4,1024,288]{1,2,0:T(8,128)}) %all-reduce.3.cloned.1.call-update) | async-done | bytes 4718608 | tf_op jit(solution)/shard_map/psum | solution.py:52
  388.9 144.1 %all-reduce.5.cloned.1.call-done = f32[4,1024,288]{1,2,0:T(8,128)} async-done(((f32[4,1024,288]{1,2,0:T(8,128)}), f32[4,1024,288]{1,2,0:T(8,128)}) %all-reduce.5.cloned.1.call-update) | async-done | bytes 4718608 | tf_op jit(solution)/shard_map/psum | solution.py:53
  533.0 3.9 multiply_convert_fusion
  537.2 1.4 fusion.35
  538.6 1.4 fusion.33
  540.0 1.4 fusion.31
  541.3 1.4 fusion.29
  542.7 1.4 fusion.27
  544.1 1.6 copy-done.9
  (30 shorter events, 5.0 us)
Async XLA Ops:
  7.2 110.2 %copy-start = (bf16[2,128,2304]{2,1,0:T(8,128)(2,1)S(1)}, bf16[2,128,2304]{2,1,0:T(8,128)(2,1)}, u32[]{:S(2)}) copy-start(bf16[2,128,2304]{2,1,0:T(8,128)(2,1)} %param.9) | copy-start | bytes 3538948
  7.2 110.2 %all-gather.3.cloned.1.call-start = ((), (), s32[]{:S(2)}) async-start(), calls=%async_computation | async-start | bytes 10616832 | tf_op jit(solution)/shard_map/all_gather | solution.py:28
  7.9 174.4 %all-gather.5.cloned.1.call-start = ((), (), s32[]{:S(2)}) async-start(), calls=%async_computation.1 | async-start | bytes 4718592 | tf_op jit(solution)/shard_map/all_gather | solution.py:32
  124.7 65.0 %copy-start.5 = (s32[10]{0:T(128)S(1)}, s32[10]{0:T(128)}, u32[]{:S(2)}) copy-start(s32[10]{0:T(128)} %constant.92.clone) | copy-start | bytes 124
  124.7 65.0 %copy-start.6 = (s32[10]{0:T(128)S(1)}, s32[10]{0:T(128)}, u32[]{:S(2)}) copy-start(s32[10]{0:T(128)} %constant.93.clone) | copy-start | bytes 124
  124.7 263.5 %all-reduce.3.cloned.1.call-start = ((), (), s32[]{:S(2)}) async-start(), calls=%async_computation.2 | async-start | bytes 9437184 | tf_op jit(solution)/shard_map/psum | solution.py:52
  185.4 44.5 %collective-permute-start = (bf16[1024,1024]{0,1:T(8,128)(2,1)}, bf16[1024,1024]{0,1:T(8,128)(2,1)S(1)}, u32[]{:S(2)}, u32[]{:S(2)}) collective-permute-start(bf16[1024,1024]{0,1:T(8,128)(2,1)} %slice_bitcast_fusion), channel_id=1, source_target_pairs={{0,128},{1,129},{2,130},{3,131},{4,132},{5,133},{6,134},{7,135},{8... | collective-permute-start | bytes 6291464 | tf_op jit(solution)/shard_map/ppermute | solution.py:10
  229.9 3.8 copy-start.1
  233.7 4.7 copy-start.3
  251.5 281.5 %all-reduce.5.cloned.1.call-start = ((), (), s32[]{:S(2)}) async-start(), calls=%async_computation.3 | async-start | bytes 9437184 | tf_op jit(solution)/shard_map/psum | solution.py:53
  388.2 0.7 copy-start.8
  388.2 144.8 %copy-start.7 = (f32[4,288]{1,0:T(4,128)S(1)}, f32[4,288]{1,0:T(4,128)}, u32[]{:S(2)}) copy-start(f32[4,288]{1,0:T(4,128)} %param.13) | copy-start | bytes 13828
  533.0 4.2 copy-start.2
  537.2 5.5 copy-start.4
  544.1 1.6 copy-start.9
Sparse Core Ops, SparseCore 0:
  9.8 107.5 all-gather.2
  124.8 57.5 all-gather.4
  251.6 136.5 all-reduce.2
  390.7 142.2 all-reduce.4
